TPU v7x, 32 devices: a whole 2x2x4 slice. The times are simulated.
32 devices in a mesh: role: 2 (over x), grp: 2 (over y), tp: 8 (over z, core).
Axes of the slice: x: 2, y: 2, z: 4, core: 2. Of those that a mesh axis runs over, the one named last changes fastest.
Arguments:
- queries: bfloat16 [2, 8, 8192], P(None, None, ('grp', 'tp')), may hold values from -130 to 130
- step_token_keys: bfloat16 [2, 8, 1024], replicated, may hold values from -6 to 6
- step_token_values: bfloat16 [2, 8, 1024], replicated, may hold values from -6 to 6
- stored_key_cache: bfloat16 [8, 512, 1024], P(None, ('grp', 'tp')), may hold values from -6 to 6
- stored_value_cache: bfloat16 [8, 512, 1024], P(None, ('grp', 'tp')), may hold values from -6 to 6
- lengths: int32 [8], replicated, may hold values from 2 to 512
- wo_sides: bfloat16 [2, 8192, 8192], P('role', ('grp', 'tp')), may hold values from -1 to 1
- gain_sides: float32 [2, 8192], P('role', ('grp', 'tp')), may hold values from 0.5 to 1.5
- head: bfloat16 [8192, 64128], P(None, ('grp', 'tp')), may hold values from -8 to 8
- resid: bfloat16 [2, 8, 8192], P(None, None, ('grp', 'tp')), may hold values from -90 to 90
- actions: int32 [2, 8], replicated, may hold values from 0 to 64127
Outputs:
- log_probs: float32 [2, 8], P('role')
- normed: bfloat16 [2, 8, 8192], P('role', None, ('grp', 'tp'))
All inputs are finite; a program needn't handle non-finite values.
Results may differ from a plain program's by a relative error of at most 0.017.
Values may be sent and summed in bfloat16 or wider, within the bound.
A program may use at most 128 MiB of HBM per device.

v0:
```python
import math

import jax
import jax.numpy as jnp
from jax import lax
from jax.sharding import PartitionSpec as P

D = 8192
QUERY_HEADS = 64
KEY_VALUE_HEADS = 8
HEAD_SIZE = 128
DECODE_STEPS = 2


def from_partner(value, axis, apart):
    mask = 2**apart
    pairs = [(source, source ^ mask) for source in range(lax.axis_size(axis))]
    return lax.ppermute(value, axis, pairs)


def merged(x, axis, combine):
    everything = jax.tree.map(
        lambda part, kind: lax.all_gather(part.astype(kind), axis),
        x,
        (jnp.bfloat16, jnp.bfloat16, jnp.bfloat16),
    )

    def take(k):
        return jax.tree.map(lambda part, own: part[k].astype(own.dtype), everything, x)

    return lax.fori_loop(
        1, lax.axis_size(axis), lambda k, so_far: combine(so_far, take(k)), take(0)
    )


def soft_combine(earlier, later):
    highest = jnp.maximum(earlier[0], later[0])
    left_factor = jnp.exp(earlier[0] - highest)
    right_factor = jnp.exp(later[0] - highest)
    return (
        highest,
        earlier[1] * left_factor + later[1] * right_factor,
        earlier[2] * left_factor[..., None] + later[2] * right_factor[..., None],
    )


def on_device(
    queries,
    step_token_keys,
    step_token_values,
    stored_key_cache,
    stored_value_cache,
    lengths,
    wo_sides,
    gain_sides,
    head,
    resid,
    actions,
):
    place = lax.axis_index(("grp", "tp"))
    side_index = lax.axis_index("role")
    count_of_rows = lengths.shape[0]
    shard_length = stored_key_cache.shape[1]
    query_group_width = QUERY_HEADS // KEY_VALUE_HEADS
    logit_scale = 1.0 / math.sqrt(HEAD_SIZE)
    gathered = lax.all_gather(queries, ("grp", "tp"), axis=2, tiled=True)
    positions = place * shard_length + jnp.arange(shard_length, dtype=jnp.int32)
    valid = positions[None, :] < lengths[:, None]
    masking = valid[:, None, None, :]
    prior_keys = stored_key_cache.astype(jnp.float32).reshape(
        count_of_rows, shard_length, KEY_VALUE_HEADS, HEAD_SIZE
    )
    prior_values = stored_value_cache.astype(jnp.float32).reshape(
        count_of_rows, shard_length, KEY_VALUE_HEADS, HEAD_SIZE
    )
    weight_used, gain_used = (
        from_partner(wo_sides[0], "role", 0),
        from_partner(gain_sides[0].astype(jnp.bfloat16), "role", 0).astype(jnp.float32),
    )
    head_width = head.shape[1]
    vocab_ids = place * head_width + jnp.arange(head_width, dtype=jnp.int32)
    step_ids = jnp.arange(DECODE_STEPS, dtype=jnp.int32)
    incoming_keys = step_token_keys.astype(jnp.float32).reshape(
        DECODE_STEPS, count_of_rows, KEY_VALUE_HEADS, HEAD_SIZE
    )
    incoming_values = step_token_values.astype(jnp.float32).reshape(
        DECODE_STEPS, count_of_rows, KEY_VALUE_HEADS, HEAD_SIZE
    )
    query_matrix = lax.dynamic_index_in_dim(gathered, side_index, 0, keepdims=False)
    current_query = (
        query_matrix.astype(jnp.float32).reshape(
            count_of_rows, KEY_VALUE_HEADS, query_group_width, HEAD_SIZE
        )
        * logit_scale
    )
    scores = jnp.einsum("rkgd,rskd->rkgs", current_query, prior_keys)
    scores = jnp.where(masking, scores, -1e30)
    highest = jnp.max(scores, axis=-1)
    cache_probs = jnp.exp(scores - highest[..., None]) * masking
    totals = jnp.sum(cache_probs, axis=-1)
    weighted = jnp.einsum("rkgs,rskd->rkgd", cache_probs, prior_values)
    highest, totals, weighted = merged((highest, totals, weighted), ("grp", "tp"), soft_combine)
    fresh_live = step_ids <= side_index
    fresh_scores = jnp.einsum("rkgd,trkd->rkgt", current_query, incoming_keys)
    fresh_scores = jnp.where(fresh_live, fresh_scores, -1e30)
    overall = jnp.maximum(highest, jnp.max(fresh_scores, axis=-1))
    cache_factor = jnp.exp(highest - overall)
    fresh_probs = jnp.exp(fresh_scores - overall[..., None]) * fresh_live
    denominator = totals * cache_factor + jnp.sum(fresh_probs, axis=-1)
    mixed = weighted * cache_factor[..., None] + jnp.einsum(
        "rkgt,trkd->rkgd", fresh_probs, incoming_values
    )
    attended = (
        (mixed / denominator[..., None])
        .reshape(count_of_rows, QUERY_HEADS * HEAD_SIZE)
        .astype(jnp.bfloat16)
    )
    feature_rows = weight_used.shape[0]
    own_part = lax.dynamic_slice_in_dim(attended, place * feature_rows, feature_rows, 1)
    branch_out = lax.psum_scatter(
        jnp.dot(own_part, weight_used, preferred_element_type=jnp.float32),
        ("grp", "tp"),
        scatter_dimension=1,
        tiled=True,
    )
    resid_now = lax.dynamic_index_in_dim(resid, side_index, 0, keepdims=False)
    state = resid_now.astype(jnp.float32) + branch_out
    square_sum = lax.psum(jnp.sum(state * state, axis=-1), ("grp", "tp"))
    normed_now = (state * lax.rsqrt(square_sum[:, None] / D + 1e-05) * gain_used[None, :]).astype(
        jnp.bfloat16
    )
    logits = jnp.dot(
        lax.all_gather(normed_now, ("grp", "tp"), axis=1, tiled=True),
        head,
        preferred_element_type=jnp.float32,
    )
    local_highest = jnp.max(logits, axis=-1)
    action_now = lax.dynamic_index_in_dim(actions, side_index, 0, keepdims=False)
    is_target = vocab_ids[None, :] == action_now[:, None]
    target = jnp.sum(jnp.where(is_target, logits, 0.0), axis=-1)
    largest = lax.pmax(local_highest, ("grp", "tp"))
    exp_sum = jnp.sum(jnp.exp(logits - largest[:, None]), axis=-1)
    exp_sum, target = lax.psum((exp_sum, target), ("grp", "tp"))
    prob_now = target - largest - jnp.log(exp_sum)
    return (prob_now[None], normed_now[None])


def solution(mesh):
    in_specs = (
        P(None, None, ("grp", "tp")),
        P(),
        P(),
        P(None, ("grp", "tp"), None),
        P(None, ("grp", "tp"), None),
        P(),
        P("role", ("grp", "tp"), None),
        P("role", ("grp", "tp")),
        P(None, ("grp", "tp")),
        P(None, None, ("grp", "tp")),
        P(),
    )
    out_specs = (P("role", None), P("role", None, ("grp", "tp")))
    return jax.shard_map(
        on_device, mesh=mesh, in_specs=in_specs, out_specs=out_specs, check_vma=False
    )
```

profile of v0, /device:TPU:0, one launch (start us, length us, event | category | flops | bytes accessed | tf_op | source)
XLA Modules:
  0.0 419.3 jit_solution(16974853084178439491)
XLA Ops:
  7.2 24.6 %all_gather.20 = bf16[2,8,8192]{2,1,0:T(8,128)(2,1)S(1)} all-gather(bf16[2,8,512]{2,1,0:T(8,128)(2,1)} %param.13), channel_id=1, replica_groups=mesh['role'=2,'grp'=2,'tp'=8] {'grp','tp'}, dimensions={2}, use_global_device_ids=true | all-gather | bytes 278528 | tf_op jit(solution)/shard_map/all_gather | solution.py:66
  32.7 1.5 fusion.27
  35.2 1.6 collective-permute-start
  37.1 18.7 %all-gather.1 = bf16[128,8,8]{2,1,0:T(8,128)(2,1)S(1)} all-gather(bf16[8,8,8]{2,1,0:T(8,128)(2,1)S(1)} %fusion.14), channel_id=3, replica_groups=mesh['role'=2,'grp'=2,'tp'=8] {'grp','tp'}, dimensions={0}, use_global_device_ids=true | all-gather | bytes 17408 | tf_op jit(solution)/shard_map/all_gather | solution.py:23
  55.8 21.4 %all-gather = bf16[128,8,8]{2,1,0:T(8,128)(2,1)S(1)} all-gather(bf16[8,8,8]{2,1,0:T(8,128)(2,1)S(1)} %convert_element_type.137), channel_id=2, replica_groups=mesh['role'=2,'grp'=2,'tp'=8] {'grp','tp'}, dimensions={0}, use_global_device_ids=true | all-gather | bytes 17408 | tf_op jit(solution)/shard_map/all_gather | solution.py:23
  79.2 18.7 %while.19 = (s32[]{:T(128)}, f32[8,8,8]{2,1,0:T(8,128)S(1)}, f32[8,8,8]{2,1,0:T(8,128)S(1)}, f32[8,8,8,128]{3,2,1,0:T(8,128)S(1)}, bf16[16,8,8,8]{3,2,1,0:T(8,12...) while((s32[]{:T(128)}, f32[8,8,8]{2,1,0:T(8,128)S(1)}, ...), condition=%wide.region_3.4_spmd, body=%wide.region_2.3_spmd.sunk | while | flops 266245 | bytes 673943 | solution.py:31
  79.3 1.2 fusion.38
  80.5 1.2 fusion.38
  81.8 1.2 fusion.38
  83.0 1.2 fusion.38
  84.3 1.2 fusion.38
  85.5 1.2 fusion.38
  90.5 1.2 fusion.38
  91.7 1.2 fusion.38
  93.0 1.2 fusion.38
  98.6 119.7 %collective-permute-done = bf16[512,8192]{1,0:T(8,128)(2,1)} collective-permute-done((bf16[512,8192]{1,0:T(8,128)(2,1)}, bf16[512,8192]{1,0:T(8,128)(2,1)}, u32[]{:S(2)}, u32[]{:S(2)}) %collective-permute-start) | collective-permute-done | bytes 8388640 | tf_op jit(solution)/shard_map/ppermute | solution.py:18
  218.3 5.3 %fusion.19 = f32[8,8192]{1,0:T(8,128)} fusion(bf16[512,8192]{1,0:T(8,128)(2,1)} %collective-permute-done, bf16[8,8192]{1,0:T(8,128)(2,1)S(1)} %bitcast.72, s32[]{:T(128)S(6)} %select_n.38), kind=kOutput, calls=%fused_computation.43 | convolution fusion | flops 67108864 | bytes 8658948 | tf_op jit(solution)/shard_map/dot_general | solution.py:121
  223.6 1.6 collective-permute-start.1
  225.2 51.6 %reduce-scatter.2.cloned.1.call-done = f32[8,512]{1,0:T(8,128)} async-done(((f32[8,8192]{1,0:T(8,128)}), f32[8,512]{1,0:T(8,128)}) %reduce-scatter.2.cloned.1.call-update) | async-done | bytes 16400 | tf_op jit(solution)/shard_map/reduce_scatter | solution.py:120
  277.6 29.6 %psum.21 = f32[8]{0:T(128)S(1)} all-reduce(f32[8]{0:T(128)S(1)} %multiply_reduce_fusion), channel_id=1, replica_groups=mesh['role'=2,'grp'=2,'tp'=8] {'grp','tp'}, use_global_device_ids=true, to_apply=%region_8.9 | all-reduce | flops 8 | bytes 64 | tf_op jit(solution)/shard_map/psum | solution.py:128
  308.0 17.6 %all_gather.25 = bf16[8,8192]{1,0:T(8,128)(2,1)S(1)} all-gather(bf16[8,512]{1,0:T(8,128)(2,1)S(1)} %multiply_convert_fusion), channel_id=1, replica_groups=mesh['role'=2,'grp'=2,'tp'=8] {'grp','tp'}, dimensions={1}, use_global_device_ids=true | all-gather | bytes 139264 | tf_op jit(solution)/shard_map/all_gather | solution.py:133
  325.6 25.1 %fusion.29 = (f32[8]{0:T(128)S(1)}, f32[8,4008]{1,0:T(8,128)S(1)}) fusion(bf16[8,8192]{1,0:T(8,128)(2,1)S(1)} %all_gather.25, bf16[8192,4008]{0,1:T(8,128)(2,1)} %param.21), kind=kOutput, calls=%fused_computation.59 | convolution fusion | flops 525368640 | bytes 65926432 | tf_op jit(solution)/shard_map/dot_general | solution.py:132
  350.8 31.4 %pmax.7 = f32[8]{0:T(128)S(1)} all-reduce(f32[8]{0:T(128)S(1)} %get-tuple-element.213), channel_id=1, replica_groups=mesh['role'=2,'grp'=2,'tp'=8] {'grp','tp'}, use_global_device_ids=true, to_apply=%region_12.13 | all-reduce | flops 8 | bytes 64 | tf_op jit(solution)/shard_map/pmax | solution.py:141
  382.5 29.5 %all-reduce = (f32[8]{0:T(128)S(1)}, f32[8]{0:T(128)S(1)}) all-reduce(f32[8]{0:T(128)S(1)} %get-tuple-element.184, f32[8]{0:T(128)S(1)} %get-tuple-element.183), channel_id=1, replica_groups=mesh['role'=2,'grp'=2,'tp'=8] {'grp','tp'}, use_global_device_ids=true, to_apply=%region_14.15 | all-reduce | flops 16 | bytes 128 | tf_op jit(solution)/shard_map/psum | solution.py:143
  (67 shorter events, 14.8 us)
Async XLA Ops:
  7.2 27.0 %copy-start = (bf16[8,32,1024]{2,1,0:T(8,128)(2,1)S(1)}, bf16[8,32,1024]{2,1,0:T(8,128)(2,1)}, u32[]{:S(2)}) copy-start(bf16[8,32,1024]{2,1,0:T(8,128)(2,1)} %param.17) | copy-start | bytes 1572868
  7.2 91.0 %copy-start.5 = (bf16[2,8,1024]{2,1,0:T(8,128)(2,1)S(1)}, bf16[2,8,1024]{2,1,0:T(8,128)(2,1)}, u32[]{:S(2)}) copy-start(bf16[2,8,1024]{2,1,0:T(8,128)(2,1)} %param.15) | copy-start | bytes 98308
  7.2 71.1 %all-gather.5.cloned.1.call-start = ((), (), s32[]{:S(2)}) async-start(), calls=%async_computation.2 | async-start | bytes 2228224 | tf_op jit(solution)/shard_map/all_gather | solution.py:23
  35.2 241.6 %reduce-scatter.2.cloned.1.call-start = ((), (), s32[]{:S(2)}) async-start(), calls=%async_computation.1 | async-start | bytes 278528 | tf_op jit(solution)/shard_map/reduce_scatter | solution.py:120
  35.2 183.1 %collective-permute-start = (bf16[512,8192]{1,0:T(8,128)(2,1)}, bf16[512,8192]{1,0:T(8,128)(2,1)}, u32[]{:S(2)}, u32[]{:S(2)}) collective-permute-start(bf16[512,8192]{1,0:T(8,128)(2,1)} %bitcast.74), channel_id=1, source_target_pairs={{0,16},{16,0},{1,17},{17,1},{2,18},{18,2},{3,19},{19,3},{4,20},{20... | collective-permute-start | bytes 25165832 | tf_op jit(solution)/shard_map/ppermute | solution.py:18
  97.9 125.7 %copy-start.4 = (f32[1,512]{1,0:T(1,128)S(1)}, f32[1,512]{1,0:T(1,128)}, u32[]{:S(2)}) copy-start(f32[1,512]{1,0:T(1,128)} %param.20) | copy-start | bytes 6148
  97.9 127.3 %copy-start.6 = (s32[2,8]{1,0:T(2,128)S(1)}, s32[2,8]{1,0:T(2,128)}, u32[]{:S(2)}) copy-start(s32[2,8]{1,0:T(2,128)} %param.23) | copy-start | bytes 196
  97.9 178.9 %copy-start.3 = (bf16[2,8,512]{2,1,0:T(8,128)(2,1)S(1)}, bf16[2,8,512]{2,1,0:T(8,128)(2,1)}, u32[]{:S(2)}) copy-start(bf16[2,8,512]{2,1,0:T(8,128)(2,1)} %param.22) | copy-start | bytes 49156
  223.6 54.0 %collective-permute-start.1 = (bf16[512]{0:T(512)(128)(2,1)S(1)}, bf16[512]{0:T(512)(128)(2,1)S(1)}, u32[]{:S(2)}, u32[]{:S(2)}) collective-permute-start(bf16[512]{0:T(512)(128)(2,1)S(1)} %convert_reduce_fusion), channel_id=1, source_target_pairs={{0,16},{16,0},{1,17},{17,1},{2,18},{18,2},{3,19},{19,3},{4,20},{20... | collective-permute-start | bytes 3080 | tf_op jit(solution)/shard_map/ppermute | solution.py:18
  308.0 42.7 %copy-start.2 = (bf16[8,512]{1,0:T(8,128)(2,1)}, bf16[8,512]{1,0:T(8,128)(2,1)S(1)}, u32[]{:S(2)}) copy-start(bf16[8,512]{1,0:T(8,128)(2,1)S(1)} %multiply_convert_fusion) | copy-start | bytes 24580
  325.6 86.8 %copy-start.1 = (bf16[8,32,1024]{2,1,0:T(8,128)(2,1)S(1)}, bf16[8,32,1024]{2,1,0:T(8,128)(2,1)}, u32[]{:S(2)}) copy-start(bf16[8,32,1024]{2,1,0:T(8,128)(2,1)} %param.17) | copy-start | bytes 1572868
Sparse Core Ops, SparseCore 0:
  35.3 39.6 all-gather.4
  223.7 52.9 reduce-scatter.1
where the time goes:
time: 420 us; the launch traced here: 419 us
  blocking collectives  173 us (41%)
  waiting for transfers between devices  171 us (41%)
  matrix products  34.2 us (8%)
  other arithmetic  22.8 us (5%)
  between operations  14.2 us (3%)
    ppermute x2, waiting for transfers between devices, from_partner(): return lax.ppermute(value, axis, pairs)  120 us
    reduce_scatter x1, waiting for transfers between devices, on_device(): lax.psum_scatter(jnp.dot(own_part, weight_used, preferred_element_type=jn...  51.6 us
    all_gather x2, blocking collectives, merged(): lax.all_gather(part.astype(kind), axis)  40.2 us
    pmax x1, blocking collectives, on_device(): largest = lax.pmax(local_highest, ('grp', 'tp'))  31.4 us
    psum x1, blocking collectives, on_device(): square_sum = lax.psum(jnp.sum(state * state, axis=-1), ('grp', 'tp'))  29.6 us
    psum x1, blocking collectives, on_device(): exp_sum, target = lax.psum((exp_sum, target), ('grp', 'tp'))  29.5 us
    dot_general x1, matrix products, on_device(): jnp.dot(lax.all_gather(normed_now, ('grp', 'tp'), axis=1, tiled=True), he...  25.1 us
    all_gather x1, blocking collectives, on_device(): gathered = lax.all_gather(queries, ('grp', 'tp'), axis=2, tiled=True)  24.6 us
  transfers between devices with their start and end apart: 4, of which 2 were waited for; matrix products, arithmetic and copies ran while one was open for 5% of the time, Pallas kernels for 0%

commit v1 on v0

v1 whole, which is shorter than its diff:
```python
import math

import jax
import jax.numpy as jnp
from jax import lax
from jax.sharding import PartitionSpec as P

D = 8192
QUERY_HEADS = 64
KEY_VALUE_HEADS = 8
HEAD_SIZE = 128
DECODE_STEPS = 2


def swap_sides(value):
    return lax.ppermute(value, "role", [(0, 1), (1, 0)])


def on_device(
    queries,
    step_token_keys,
    step_token_values,
    stored_key_cache,
    stored_value_cache,
    lengths,
    wo_sides,
    gain_sides,
    head,
    resid,
    actions,
):
    both = ("grp", "tp")
    place = lax.axis_index(both)
    step = 1 - lax.axis_index("role")
    count_of_rows = lengths.shape[0]
    shard_length = stored_key_cache.shape[1]
    query_group_width = QUERY_HEADS // KEY_VALUE_HEADS
    logit_scale = 1.0 / math.sqrt(HEAD_SIZE)
    query_matrix = lax.all_gather(
        lax.dynamic_index_in_dim(queries, step, 0, keepdims=False), both, axis=1, tiled=True
    )
    positions = place * shard_length + jnp.arange(shard_length, dtype=jnp.int32)
    valid = positions[None, :] < lengths[:, None]
    masking = valid[:, None, None, :]
    cache_shape = (count_of_rows, shard_length, KEY_VALUE_HEADS, HEAD_SIZE)
    prior_keys = stored_key_cache.reshape(cache_shape)
    prior_values = stored_value_cache.reshape(cache_shape)
    step_shape = (DECODE_STEPS, count_of_rows, KEY_VALUE_HEADS, HEAD_SIZE)
    incoming_keys = step_token_keys.astype(jnp.float32).reshape(step_shape)
    incoming_values = step_token_values.astype(jnp.float32).reshape(step_shape)
    current_query = query_matrix.reshape(
        count_of_rows, KEY_VALUE_HEADS, query_group_width, HEAD_SIZE
    )
    scores = (
        jnp.einsum("rkgd,rskd->rkgs", current_query, prior_keys, preferred_element_type=jnp.float32)
        * logit_scale
    )
    scores = jnp.where(masking, scores, -1e30)
    fresh_live = jnp.arange(DECODE_STEPS, dtype=jnp.int32) <= step
    fresh_scores = (
        jnp.einsum("rkgd,trkd->rkgt", current_query.astype(jnp.float32), incoming_keys)
        * logit_scale
    )
    fresh_scores = jnp.where(fresh_live, fresh_scores, -1e30)
    fresh_highest = jnp.max(fresh_scores, axis=-1)
    overall = lax.pmax(jnp.maximum(jnp.max(scores, axis=-1), fresh_highest), both)
    cache_probs = jnp.exp(scores - overall[..., None]) * masking
    fresh_probs = jnp.exp(fresh_scores - overall[..., None]) * fresh_live
    fresh_probs = fresh_probs * (place == 0)
    totals = jnp.sum(cache_probs, axis=-1) + jnp.sum(fresh_probs, axis=-1)
    weighted = jnp.einsum(
        "rkgs,rskd->rkgd", cache_probs, prior_values.astype(jnp.float32)
    ) + jnp.einsum("rkgt,trkd->rkgd", fresh_probs, incoming_values)
    features = QUERY_HEADS * HEAD_SIZE
    mixed = lax.psum_scatter(
        weighted.reshape(count_of_rows, features), both, scatter_dimension=1, tiled=True
    )
    totals = lax.psum(totals.reshape(count_of_rows, QUERY_HEADS), both)
    feature_rows = wo_sides.shape[1]
    own_heads = (place * feature_rows + jnp.arange(feature_rows)) // HEAD_SIZE
    own_part = (mixed / jnp.take(totals, own_heads, axis=1)).astype(jnp.bfloat16)
    branch_out = lax.psum_scatter(
        jnp.dot(own_part, wo_sides[0], preferred_element_type=jnp.float32),
        both,
        scatter_dimension=1,
        tiled=True,
    )
    resid_now = lax.dynamic_index_in_dim(resid, step, 0, keepdims=False)
    state = resid_now.astype(jnp.float32) + branch_out
    square_sum = lax.psum(jnp.sum(state * state, axis=-1), both)
    normed_now = (
        state * lax.rsqrt(square_sum[:, None] / D + 1e-05) * gain_sides[0][None, :]
    ).astype(jnp.bfloat16)
    logits = jnp.dot(
        lax.all_gather(normed_now, both, axis=1, tiled=True),
        head,
        preferred_element_type=jnp.float32,
    )
    local_highest = jnp.max(logits, axis=-1)
    action_now = lax.dynamic_index_in_dim(actions, step, 0, keepdims=False)
    head_width = head.shape[1]
    vocab_ids = place * head_width + jnp.arange(head_width, dtype=jnp.int32)
    is_target = vocab_ids[None, :] == action_now[:, None]
    target = jnp.sum(jnp.where(is_target, logits, 0.0), axis=-1)
    exp_sum = jnp.sum(jnp.exp(logits - local_highest[:, None]), axis=-1)
    parts = lax.all_gather(jnp.stack([local_highest, exp_sum, target]), both)
    largest = jnp.max(parts[:, 0], axis=0)
    exp_sum = jnp.sum(parts[:, 1] * jnp.exp(parts[:, 0] - largest[None]), axis=0)
    prob_now = jnp.sum(parts[:, 2], axis=0) - largest - jnp.log(exp_sum)
    return (swap_sides(prob_now)[None], swap_sides(normed_now)[None])


def solution(mesh):
    in_specs = (
        P(None, None, ("grp", "tp")),
        P(),
        P(),
        P(None, ("grp", "tp"), None),
        P(None, ("grp", "tp"), None),
        P(),
        P("role", ("grp", "tp"), None),
        P("role", ("grp", "tp")),
        P(None, ("grp", "tp")),
        P(None, None, ("grp", "tp")),
        P(),
    )
    out_specs = (P("role", None), P("role", None, ("grp", "tp")))
    return jax.shard_map(
        on_device, mesh=mesh, in_specs=in_specs, out_specs=out_specs, check_vma=False
    )
```

time: 420 us -> 335 us (0.80)
  waiting for transfers between devices: 171 us -> 67.8 us
  blocking collectives: 173 us -> 207 us
  other arithmetic: 22.8 us -> 3.38 us
  local copies, waits for them, and re-layouts: 0.14 us -> 5.74 us
    ppermute x2, waiting for transfers between devices: 120 us -> 2.93 us  [swap_sides(): return lax.ppermute(value, 'role', [(0, 1), (1, 0)])]
    psum x2, blocking collectives: 59.1 us -> 88.2 us  [the longest x1 58.6 us: on_device(): totals = lax.psum(totals.reshape(count_of_rows, QUERY_HEADS), both)]
    pmax x1, blocking collectives: 31.4 us -> 57.8 us  [on_device(): lax.pmax(jnp.maximum(jnp.max(scores, axis=-1), fresh_highest), both)]
    all_gather x4 -> x3, blocking collectives: 82.4 us -> 60.6 us  [the longest x1 23.8 us: on_device(): lax.all_gather(lax.dynamic_index_in_dim(queries, step, 0, keepdims=False)...]
    add x31 -> x1, other arithmetic: 18.2 us -> 0.01 us  [on_device(): totals = jnp.sum(cache_probs, axis=-1) + jnp.sum(fresh_probs, axis=-1)]
    reduce_scatter x1 -> x2, waiting for transfers between devices: 51.6 us -> 64.8 us  [the longest x1 54.9 us: on_device(): lax.psum_scatter(jnp.dot(own_part, wo_sides[0], preferred_element_type=jn...]
  transfers between devices with their start and end apart: 4 -> 4, of which waited for: 2 -> 3; matrix products, arithmetic and copies ran while one was open for 5% -> 8% of each run, Pallas kernels for 0% -> 0%
where the time goes in v1:
time: 335 us; the launch traced here: 334 us
  blocking collectives  207 us (62%)
  waiting for transfers between devices  67.8 us (20%)
  matrix products  34.5 us (10%)
  between operations  14.2 us (4%)
  local copies, waits for them, and re-layouts  5.74 us (2%)
  other arithmetic  3.38 us (1%)
    psum x1, blocking collectives, on_device(): totals = lax.psum(totals.reshape(count_of_rows, QUERY_HEADS), both)  58.6 us
    pmax x1, blocking collectives, on_device(): lax.pmax(jnp.maximum(jnp.max(scores, axis=-1), fresh_highest), both)  57.8 us
    reduce_scatter x1, waiting for transfers between devices, on_device(): lax.psum_scatter(jnp.dot(own_part, wo_sides[0], preferred_element_type=jn...  54.9 us
    psum x1, blocking collectives, on_device(): square_sum = lax.psum(jnp.sum(state * state, axis=-1), both)  29.6 us
    dot_general x1, matrix products, on_device(): jnp.dot(lax.all_gather(normed_now, both, axis=1, tiled=True), head, prefe...  25.1 us
    all_gather x1, blocking collectives, on_device(): lax.all_gather(lax.dynamic_index_in_dim(queries, step, 0, keepdims=False)...  23.8 us
    all_gather x1, blocking collectives, on_device(): parts = lax.all_gather(jnp.stack([local_highest, exp_sum, target]), both)  19.2 us
    all_gather x1, blocking collectives, on_device(): lax.all_gather(normed_now, both, axis=1, tiled=True)  17.6 us
  transfers between devices with their start and end apart: 4, of which 3 were waited for; matrix products, arithmetic and copies ran while one was open for 8% of the time, Pallas kernels for 0%

profile of v1, /device:TPU:0, one launch (start us, length us, event | category | flops | bytes accessed | tf_op | source)
XLA Modules:
  0.0 334.4 jit_solution(1185323969059344830)
XLA Ops:
  7.3 0.7 constant_dynamic-slice_fusion.1
  8.0 23.8 %all-gather = bf16[1,8,8192]{2,1,0:T(8,128)(2,1)S(1)} all-gather(bf16[1,8,512]{2,1,0:T(8,128)(2,1)S(1)} %constant_dynamic-slice_fusion.1), channel_id=2, replica_groups=mesh['role'=2,'grp'=2,'tp'=8] {'grp','tp'}, dimensions={2}, use_global_device_ids=true | all-gather | bytes 139264 | tf_op jit(solution)/shard_map/all_gather | solution.py:39
  31.8 0.7 fusion.31
  32.5 1.0 fusion.34
  33.5 1.5 fusion.33
  35.0 57.8 %pmax.7 = f32[8,8,8]{2,1,0:T(8,128)S(1)} all-reduce(f32[8,8,8]{2,1,0:T(8,128)S(1)} %max.5), channel_id=1, replica_groups=mesh['role'=2,'grp'=2,'tp'=8] {'grp','tp'}, use_global_device_ids=true, to_apply=%region_2.3 | all-reduce | flops 512 | bytes 4096 | tf_op jit(solution)/shard_map/pmax | solution.py:66
  92.8 1.1 fusion.19
  94.3 2.6 copy.35
  97.5 58.6 %psum.14 = f32[8,64]{0,1:T(8,128)S(1)} all-reduce(f32[8,64]{0,1:T(8,128)S(1)} %bitcast.70), channel_id=1, replica_groups=mesh['role'=2,'grp'=2,'tp'=8] {'grp','tp'}, use_global_device_ids=true, to_apply=%region_6.7 | all-reduce | flops 512 | bytes 4096 | tf_op jit(solution)/shard_map/psum | solution.py:78
  156.1 1.0 gather_fusion
  157.2 9.9 %reduce-scatter.3.cloned.1.call-done = f32[8,512]{0,1:T(8,128)} async-done(((f32[8,8192]{0,1:T(8,128)}), f32[8,512]{0,1:T(8,128)}) %reduce-scatter.3.cloned.1.call-update) | async-done | bytes 16400 | tf_op jit(solution)/shard_map/reduce_scatter | solution.py:75
  167.1 5.5 %fusion = f32[8,8192]{1,0:T(8,128)} fusion(bf16[1,512,8192]{2,1,0:T(8,128)(2,1)} %param.17, f32[8,512]{0,1:T(8,128)} %reduce-scatter.3.cloned.1.call-done, f32[512,8]{1,0:T(8,128)S(1)} %gather_fusion, pred[512]{0:T(512)(128)(4,1)S(1)} %compare_and_fusion), kind=kOutput, calls=%fused_computation.1 | convolution fusion | flops 67121152 | bytes 8684032 | tf_op jit(solution)/shard_map/dot_general | solution.py:83
  172.7 54.9 %reduce-scatter.5.cloned.1.call-done = f32[8,512]{1,0:T(8,128)} async-done(((f32[8,8192]{1,0:T(8,128)}), f32[8,512]{1,0:T(8,128)}) %reduce-scatter.5.cloned.1.call-update) | async-done | bytes 16400 | tf_op jit(solution)/shard_map/reduce_scatter | solution.py:82
  227.6 0.8 multiply_reduce_fusion
  228.4 29.6 %psum.15 = f32[8]{0:T(128)S(1)} all-reduce(f32[8]{0:T(128)S(1)} %multiply_reduce_fusion), channel_id=1, replica_groups=mesh['role'=2,'grp'=2,'tp'=8] {'grp','tp'}, use_global_device_ids=true, to_apply=%region_9.10 | all-reduce | flops 8 | bytes 64 | tf_op jit(solution)/shard_map/psum | solution.py:90
  258.0 0.8 multiply_convert_fusion
  258.8 1.4 collective-permute-start.1
  260.2 17.6 %all_gather.13 = bf16[8,8192]{1,0:T(8,128)(2,1)S(1)} all-gather(bf16[8,512]{1,0:T(8,128)(2,1)S(1)} %multiply_convert_fusion), channel_id=1, replica_groups=mesh['role'=2,'grp'=2,'tp'=8] {'grp','tp'}, dimensions={1}, use_global_device_ids=true | all-gather | bytes 139264 | tf_op jit(solution)/shard_map/all_gather | solution.py:95
  277.8 25.1 %fusion.35 = (f32[8]{0:T(128)S(1)}, f32[8,4008]{1,0:T(8,128)S(1)}) fusion(bf16[8,8192]{1,0:T(8,128)(2,1)S(1)} %all_gather.13, bf16[8192,4008]{0,1:T(8,128)(2,1)} %param.19), kind=kOutput, calls=%fused_computation.72 | convolution fusion | flops 525368640 | bytes 65926432 | tf_op jit(solution)/shard_map/dot_general | solution.py:94
  303.2 19.2 %all-gather.2 = f32[16,3,8]{2,1,0:T(4,128)S(1)} all-gather(f32[1,3,8]{2,1,0:T(4,128)S(1)} %maximum_bitcast_fusion), channel_id=3, replica_groups=mesh['role'=2,'grp'=2,'tp'=8] {'grp','tp'}, dimensions={0}, use_global_device_ids=true | all-gather | bytes 1632 | tf_op jit(solution)/shard_map/all_gather | solution.py:106
  322.8 0.7 collective-permute-start
  323.5 2.9 collective-permute-done
  326.4 0.5 copy.72
  327.0 0.6 copy.73
  (37 shorter events, 1.7 us)
Async XLA Ops:
  7.2 86.8 %copy-start = (bf16[8,32,1024]{2,1,0:T(8,128)(2,1)S(1)}, bf16[8,32,1024]{2,1,0:T(8,128)(2,1)}, u32[]{:S(2)}) copy-start(bf16[8,32,1024]{2,1,0:T(8,128)(2,1)} %param.15) | copy-start | bytes 1572868
  7.2 160.0 %reduce-scatter.3.cloned.1.call-start = ((), (), s32[]{:S(2)}) async-start(), calls=%async_computation.2 | async-start | bytes 4456448 | tf_op jit(solution)/shard_map/reduce_scatter | solution.py:75
  96.9 130.7 %copy-start.2 = (bf16[2,8,512]{2,1,0:T(8,128)(2,1)S(1)}, bf16[2,8,512]{2,1,0:T(8,128)(2,1)}, u32[]{:S(2)}) copy-start(bf16[2,8,512]{2,1,0:T(8,128)(2,1)} %param.20) | copy-start | bytes 49156
  96.9 131.5 %copy-start.4 = (s32[2,8]{1,0:T(2,128)S(1)}, s32[2,8]{1,0:T(2,128)}, u32[]{:S(2)}) copy-start(s32[2,8]{1,0:T(2,128)} %param.21) | copy-start | bytes 196
  96.9 161.1 %copy-start.3 = (f32[1,512]{1,0:T(1,128)S(1)}, f32[1,512]{1,0:T(1,128)}, u32[]{:S(2)}) copy-start(f32[1,512]{1,0:T(1,128)} %param.18) | copy-start | bytes 6148
  96.9 130.6 %reduce-scatter.5.cloned.1.call-start = ((), (), s32[]{:S(2)}) async-start(), calls=%async_computation.3 | async-start | bytes 278528 | tf_op jit(solution)/shard_map/reduce_scatter | solution.py:82
  258.8 67.7 %collective-permute-start.1 = (bf16[8,512]{1,0:T(8,128)(2,1)S(1)}, bf16[8,512]{1,0:T(8,128)(2,1)S(1)}, u32[]{:S(2)}, u32[]{:S(2)}) collective-permute-start(bf16[8,512]{1,0:T(8,128)(2,1)S(1)} %multiply_convert_fusion), channel_id=1, source_target_pairs={{0,16},{16,0},{1,17},{17,1},{2,18},{18,2},{3,19},{19,3},{4,20},{20... | collective-permute-start | bytes 24584 | tf_op jit(solution)/shard_map/ppermute | solution.py:16
  277.8 49.7 %copy-start.1 = (bf16[8,32,1024]{2,1,0:T(8,128)(2,1)S(1)}, bf16[8,32,1024]{2,1,0:T(8,128)(2,1)}, u32[]{:S(2)}) copy-start(bf16[8,32,1024]{2,1,0:T(8,128)(2,1)} %param.15) | copy-start | bytes 1572868
  322.8 3.6 %collective-permute-start = (f32[8]{0:T(128)S(1)}, f32[8]{0:T(128)S(1)}, u32[]{:S(2)}, u32[]{:S(2)}) collective-permute-start(f32[8]{0:T(128)S(1)} %log_subtract_fusion), channel_id=1, source_target_pairs={{0,16},{16,0},{1,17},{17,1},{2,18},{18,2},{3,19},{19,3},{4,20},{20... | collective-permute-start | bytes 104 | tf_op jit(solution)/shard_map/ppermute | solution.py:16
Sparse Core Ops, SparseCore 0:
  97.0 70.0 reduce-scatter.2
  172.8 54.7 reduce-scatter.4

commit v2 on v1

--- a/solution.py
+++ b/solution.py
@@ -1,8 +1,11 @@
+import functools
 import math
 
 import jax
 import jax.numpy as jnp
 from jax import lax
+from jax.experimental import pallas as pl
+from jax.experimental.pallas import tpu as pltpu
 from jax.sharding import PartitionSpec as P
 
 D = 8192
@@ -16,7 +19,7 @@
     return lax.ppermute(value, "role", [(0, 1), (1, 0)])
 
 
-def on_device(
+def plain(
     queries,
     step_token_keys,
     step_token_values,
@@ -110,6 +113,532 @@
     return (swap_sides(prob_now)[None], swap_sides(normed_now)[None])
 
 
+LOW = -1e30
+TILE = 512
+MESH = pl.DeviceIdType.MESH
+
+
+def fused_kernel(
+    n,
+    tp,
+    queries,
+    token_keys,
+    token_values,
+    keys,
+    values,
+    lengths,
+    gain,
+    resid,
+    actions,
+    wo,
+    head,
+    log_probs,
+    normed,
+    wo_buf,
+    head_buf,
+    q_all,
+    b_send,
+    b_recv,
+    c_send,
+    c_recv,
+    d_send,
+    d_recv,
+    x_send,
+    x_recv,
+    s_send,
+    s_recv,
+    x_rows,
+    y_keep,
+    y_send,
+    y_recv,
+    e_send,
+    e_recv,
+    wo_sem,
+    head_sems,
+    q_ss,
+    q_rs,
+    b_ss,
+    b_rs,
+    c_ss,
+    c_rs,
+    d_ss,
+    d_rs,
+    x_sem,
+    s_ss,
+    s_rs,
+    y_ss,
+    y_rs,
+    e_ss,
+    e_rs,
+):
+    role = lax.axis_index("role")
+    me = lax.axis_index("grp") * tp + lax.axis_index("tp")
+    step = 1 - role
+    half = n // 2
+    rows = lengths.shape[0]
+    shard = keys.shape[1]
+    width = resid.shape[2]
+    own_heads = width // HEAD_SIZE
+    group = QUERY_HEADS // KEY_VALUE_HEADS
+    slots = rows * shard
+    depth = head_buf.shape[1]
+    vocab = head.shape[0]
+    full = vocab // TILE
+    tail = vocab - full * TILE
+    tiles = y_keep.shape[0]
+    scale = 1.0 / math.sqrt(HEAD_SIZE)
+    f32 = jnp.float32
+    bf16 = jnp.bfloat16
+
+    def device(side, place):
+        return (side, place // tp, place % tp)
+
+    def remote(src, dst, ss, rs, side, place):
+        return pltpu.make_async_remote_copy(
+            src_ref=src,
+            dst_ref=dst,
+            send_sem=ss,
+            recv_sem=rs,
+            device_id=device(side, place),
+            device_id_type=MESH,
+        )
+
+    wo_copy = pltpu.make_async_copy(wo.at[0], wo_buf, wo_sem)
+    wo_copy.start()
+
+    def head_copy(first, size, sem):
+        return pltpu.make_async_copy(
+            head.at[pl.ds(first, size), pl.ds(pl.multiple_of(role * depth, 128), depth)],
+            head_buf.at[pl.ds(first, size), :],
+            sem,
+        )
+
+    @pl.loop(0, full)
+    def _(j):
+        head_copy(pl.multiple_of(j * TILE, TILE), TILE, head_sems.at[j]).start()
+
+    if tail:
+        head_copy(full * TILE, tail, head_sems.at[full]).start()
+
+    barrier = pltpu.get_barrier_semaphore()
+
+    @pl.loop(1, 2 * n)
+    def _(i):
+        other = (role * n + me + i) % (2 * n)
+        pl.semaphore_signal(
+            barrier, inc=1, device_id=device(other // n, other % n), device_id_type=MESH
+        )
+
+    pl.semaphore_wait(barrier, 2 * n - 1)
+
+    @pl.loop(1, n)
+    def _(i):
+        to = (me + i) % n
+        remote(queries.at[step], q_all.at[me], q_ss.at[i], q_rs.at[me], role, to).start()
+
+    q_all[me] = queries[step]
+
+    row_ids = lax.broadcasted_iota(jnp.int32, (group * rows, slots), 0) % rows
+    col_ids = lax.broadcasted_iota(jnp.int32, (group * rows, slots), 1)
+    limit = jnp.zeros((group * rows, slots), jnp.int32)
+    for b in range(rows):
+        limit = jnp.where(row_ids == b, lengths[b], limit)
+    place_ids = me * shard + col_ids % shard
+    live = (col_ids // shard == row_ids) & (place_ids < limit)
+
+    @pl.loop(1, n)
+    def _(i):
+        src = (me + i) % n
+        remote(queries.at[step], q_all.at[src], q_ss.at[i], q_rs.at[src], role, me).wait_recv()
+
+    lane = lax.broadcasted_iota(jnp.int32, (rows, HEAD_SIZE), 1)
+    per_group = group // own_heads
+    for k in range(KEY_VALUE_HEADS):
+        lanes = slice(k * HEAD_SIZE, (k + 1) * HEAD_SIZE)
+        query = jnp.concatenate(
+            [
+                q_all[
+                    k * per_group + h // own_heads,
+                    :,
+                    (h % own_heads) * HEAD_SIZE : (h % own_heads + 1) * HEAD_SIZE,
+                ].astype(f32)
+                for h in range(group)
+            ],
+            axis=0,
+        ).astype(bf16)
+        key = keys[:, :, lanes].reshape(slots, HEAD_SIZE)
+        value = values[:, :, lanes].reshape(slots, HEAD_SIZE)
+        scores = (
+            lax.dot_general(query, key, (((1,), (1,)), ((), ())), preferred_element_type=f32)
+            * scale
+        )
+        scores = jnp.where(live, scores, LOW)
+        top = jnp.max(scores, axis=1, keepdims=True).astype(bf16).astype(f32)
+        probs = jnp.where(live, jnp.exp(scores - top), 0.0).astype(bf16)
+        total = jnp.sum(probs.astype(f32), axis=1, keepdims=True)
+        total_high = total.astype(bf16).astype(f32)
+        total_low = total - total_high
+        weighted = jnp.dot(probs, value, preferred_element_type=f32)
+        for part in range(per_group):
+            to = k * per_group + part
+            stats = jnp.zeros((rows, HEAD_SIZE), f32)
+            for j in range(own_heads):
+                at = (part * own_heads + j) * rows
+                stats = jnp.where(lane == j, top[at : at + rows], stats)
+                stats = jnp.where(lane == own_heads + j, total_high[at : at + rows], stats)
+                stats = jnp.where(lane == 2 * own_heads + j, total_low[at : at + rows], stats)
+            first = part * own_heads * rows
+            b_send[to] = jnp.concatenate(
+                [weighted[first : first + own_heads * rows], stats, jnp.zeros_like(stats)], axis=0
+            ).astype(bf16)
+
+    @pl.loop(1, n)
+    def _(i):
+        to = (me + i) % n
+        remote(b_send.at[to], b_recv.at[me], b_ss.at[i], b_rs.at[me], role, to).start()
+
+    b_recv[me] = b_send[me]
+
+    kv_lanes = pl.ds(pl.multiple_of((me // per_group) * HEAD_SIZE, HEAD_SIZE), HEAD_SIZE)
+    own_query = queries[step].astype(f32)
+    fresh = []
+    fresh_values = []
+    for u in range(DECODE_STEPS):
+        fresh_key = token_keys[u, :, kv_lanes].astype(f32)
+        fresh_values.append(token_values[u, :, kv_lanes].astype(f32))
+        fresh.append(
+            [
+                jnp.where(
+                    u <= step,
+                    jnp.sum(
+                        own_query[:, j * HEAD_SIZE : (j + 1) * HEAD_SIZE] * fresh_key,
+                        axis=1,
+                        keepdims=True,
+                    )
+                    * scale,
+                    LOW,
+                )
+                for j in range(own_heads)
+            ]
+        )
+
+    @pl.loop(1, n)
+    def _(i):
+        src = (me + i) % n
+        remote(b_send.at[src], b_recv.at[src], b_ss.at[i], b_rs.at[src], role, me).wait_recv()
+
+    stat_rows = slice(own_heads * rows, own_heads * rows + 16)
+    stats = [b_recv[s, stat_rows, :].astype(f32)[:rows] for s in range(n)]
+    top = functools.reduce(jnp.maximum, stats)
+    tops = [
+        functools.reduce(
+            jnp.maximum, [fresh[u][j] for u in range(DECODE_STEPS)], top[:, j : j + 1]
+        )
+        for j in range(own_heads)
+    ]
+    numerator = [jnp.zeros((rows, HEAD_SIZE), f32) for _ in range(own_heads)]
+    denominator = [jnp.zeros((rows, 1), f32) for _ in range(own_heads)]
+    for j in range(own_heads):
+        for u in range(DECODE_STEPS):
+            weight = jnp.where(u <= step, jnp.exp(fresh[u][j] - tops[j]), 0.0)
+            numerator[j] += weight * fresh_values[u]
+            denominator[j] += weight
+    for s in range(n):
+        part = b_recv[s, : own_heads * rows, :].astype(f32)
+        for j in range(own_heads):
+            factor = jnp.exp(stats[s][:, j : j + 1] - tops[j])
+            numerator[j] += factor * part[j * rows : (j + 1) * rows]
+            at = own_heads + j
+            denominator[j] += factor * (
+                stats[s][:, at : at + 1] + stats[s][:, at + own_heads : at + own_heads + 1]
+            )
+    attended = jnp.concatenate(
+        [numerator[j] / denominator[j] for j in range(own_heads)], axis=1
+    ).astype(bf16)
+
+    wo_copy.wait()
+
+    def project(to):
+        return jnp.dot(
+            attended,
+            wo_buf[:, pl.ds(pl.multiple_of(to * width, 128), width)],
+            preferred_element_type=f32,
+        )
+
+    @pl.loop(1, n)
+    def _(i):
+        to = (me + i) % n
+        c_send[to] = project(to).astype(bf16)
+        remote(c_send.at[to], c_recv.at[me], c_ss.at[i], c_rs.at[me], role, to).start()
+
+    c_recv[me] = jnp.zeros((rows, width), bf16)
+    state = resid[step].astype(f32) + project(me)
+
+    @pl.loop(1, n)
+    def _(i):
+        src = (me + i) % n
+        remote(c_send.at[src], c_recv.at[src], c_ss.at[i], c_rs.at[src], role, me).wait_recv()
+
+    for s in range(n):
+        state += c_recv[s].astype(f32)
+
+    x = state * gain[...]
+    d_send[...] = x.astype(bf16)
+    x_send[...] = x
+    s_send[...] = jnp.broadcast_to(jnp.sum(state * state, axis=1, keepdims=True), (rows, HEAD_SIZE))
+    target_role = me // half
+    own_slot = role * half + me % half
+
+    @pl.when(target_role != role)
+    def _():
+        remote(
+            d_send, d_recv.at[own_slot], d_ss.at[0], d_rs.at[own_slot], target_role, me
+        ).start()
+
+    @pl.when(target_role == role)
+    def _():
+        d_recv[own_slot] = d_send[...]
+
+    @pl.loop(1, n)
+    def _(i):
+        to = (me + i) % n
+        remote(
+            d_send, d_recv.at[own_slot], d_ss.at[i], d_rs.at[own_slot], target_role, to
+        ).start()
+
+    @pl.loop(0, n)
+    def _(i):
+        to = (me + i) % n
+        remote(s_send, s_recv.at[me], s_ss.at[i], s_rs.at[me], 1 - role, to).start()
+
+    remote(x_send, x_recv, x_sem.at[0], x_sem.at[1], 1 - role, me).start()
+
+    @pl.loop(0, n)
+    def _(slot):
+        mine = (slot // half == role) & (role * half + slot % half == me)
+
+        @pl.when(jnp.logical_not(mine))
+        def _():
+            remote(d_send, d_recv.at[slot], d_ss.at[0], d_rs.at[slot], role, me).wait_recv()
+
+    for f in range(half):
+        x_rows[:, f * width : (f + 1) * width] = jnp.concatenate(
+            [d_recv[half + f].astype(f32), d_recv[f].astype(f32)], axis=0
+        ).astype(bf16)
+
+    def vocab_dot(block):
+        return lax.dot_general(
+            x_rows[...], block, (((1,), (1,)), ((), ())), preferred_element_type=f32
+        )
+
+    def y_copy(j):
+        return remote(y_send.at[j], y_recv.at[j], y_ss.at[j], y_rs.at[j], 1 - role, me)
+
+    @pl.loop(0, full)
+    def _(j):
+        first = pl.multiple_of(j * TILE, TILE)
+        head_copy(first, TILE, head_sems.at[j]).wait()
+        y = vocab_dot(head_buf[pl.ds(first, TILE), :])
+        y_keep[j] = jnp.where(role == 0, y[:rows], y[rows:])
+        y_send[j] = jnp.where(role == 0, y[rows:], y[:rows])
+        y_copy(j).start()
+
+    if tail:
+        head_copy(full * TILE, tail, head_sems.at[full]).wait()
+        y = vocab_dot(head_buf[full * TILE :, :])
+        y_keep[full] = jnp.zeros((rows, TILE), f32)
+        y_send[full] = jnp.zeros((rows, TILE), f32)
+        y_keep[full, :, :tail] = jnp.where(role == 0, y[:rows], y[rows:])
+        y_send[full, :, :tail] = jnp.where(role == 0, y[rows:], y[:rows])
+        y_copy(full).start()
+
+    @pl.loop(0, n)
+    def _(s):
+        remote(s_send, s_recv.at[s], s_ss.at[s], s_rs.at[s], role, me).wait_recv()
+
+    square_sum = jnp.zeros((rows, HEAD_SIZE), f32)
+    for s in range(n):
+        square_sum += s_recv[s]
+    inverse = lax.rsqrt(square_sum / (n * width) + 1e-05)[:, :1]
+    remote(x_send, x_recv, x_sem.at[0], x_sem.at[1], role, me).wait_recv()
+    normed[0] = (x_recv[...] * inverse).astype(bf16)
+
+    action_rows = lax.broadcasted_iota(jnp.int32, (rows, 1), 0)
+    action = jnp.zeros((rows, 1), jnp.int32)
+    for b in range(rows):
+        action = jnp.where(action_rows == b, actions[role, b], action)
+    tile_ids = lax.broadcasted_iota(jnp.int32, (rows, TILE), 1)
+    logits = []
+    for j in range(tiles):
+        y_copy(j).wait_recv()
+        tile = (y_keep[j] + y_recv[j]) * inverse
+        if j == full:
+            tile = jnp.where(tile_ids < tail, tile, LOW)
+        logits.append(tile)
+    largest = jnp.max(functools.reduce(jnp.maximum, logits), axis=1, keepdims=True)
+    exp_sum = jnp.zeros((rows, TILE), f32)
+    target = jnp.zeros((rows, TILE), f32)
+    for j in range(tiles):
+        exp_sum += jnp.exp(logits[j] - largest)
+        here = tile_ids + j * TILE == action - me * vocab
+        if j == full:
+            here = here & (tile_ids < tail)
+        target += jnp.where(here, logits[j], 0.0)
+    exp_sum = jnp.sum(exp_sum, axis=1, keepdims=True)
+    target = jnp.sum(target, axis=1, keepdims=True)
+    e_send[...] = jnp.where(lane == 0, largest, jnp.where(lane == 1, exp_sum, target))
+
+    @pl.loop(1, n)
+    def _(i):
+        to = (me + i) % n
+        remote(e_send, e_recv.at[me], e_ss.at[i], e_rs.at[me], role, to).start()
+
+    e_recv[me] = e_send[...]
+
+    @pl.loop(1, n)
+    def _(i):
+        src = (me + i) % n
+        remote(e_send, e_recv.at[src], e_ss.at[i], e_rs.at[src], role, me).wait_recv()
+
+    top = functools.reduce(jnp.maximum, [e_recv[s] for s in range(n)])[:, :1]
+    exp_sum = jnp.zeros((rows, 1), f32)
+    target = jnp.zeros((rows, 1), f32)
+    for s in range(n):
+        got = e_recv[s]
+        exp_sum += got[:, 1:2] * jnp.exp(got[:, :1] - top)
+        target += got[:, 2:3]
+    result = jnp.broadcast_to(target - top - jnp.log(exp_sum), (rows, HEAD_SIZE))
+    diagonal = lax.broadcasted_iota(jnp.int32, (rows, HEAD_SIZE), 0) == lane
+    log_probs[...] = jnp.sum(jnp.where(diagonal, result, 0.0), axis=0, keepdims=True)[:, :rows]
+
+    @pl.loop(1, n)
+    def _(i):
+        to = (me + i) % n
+        remote(queries.at[step], q_all.at[me], q_ss.at[i], q_rs.at[me], role, to).wait_send()
+        remote(b_send.at[to], b_recv.at[me], b_ss.at[i], b_rs.at[me], role, to).wait_send()
+        remote(c_send.at[to], c_recv.at[me], c_ss.at[i], c_rs.at[me], role, to).wait_send()
+        remote(
+            d_send, d_recv.at[own_slot], d_ss.at[i], d_rs.at[own_slot], target_role, to
+        ).wait_send()
+        remote(e_send, e_recv.at[me], e_ss.at[i], e_rs.at[me], role, to).wait_send()
+
+    @pl.when(target_role != role)
+    def _():
+        remote(
+            d_send, d_recv.at[own_slot], d_ss.at[0], d_rs.at[own_slot], target_role, me
+        ).wait_send()
+
+    @pl.loop(0, n)
+    def _(i):
+        remote(s_send, s_recv.at[me], s_ss.at[i], s_rs.at[me], 1 - role, me).wait_send()
+
+    remote(x_send, x_recv, x_sem.at[0], x_sem.at[1], 1 - role, me).wait_send()
+    for j in range(tiles):
+        y_copy(j).wait_send()
+
+
+def fused(
+    queries,
+    step_token_keys,
+    step_token_values,
+    stored_key_cache,
+    stored_value_cache,
+    lengths,
+    wo_sides,
+    gain_sides,
+    head,
+    resid,
+    actions,
+):
+    tp = lax.axis_size("tp")
+    n = lax.axis_size("grp") * tp
+    rows = lengths.shape[0]
+    width = resid.shape[2]
+    heads = width // HEAD_SIZE
+    depth = head.shape[0] // 2
+    tiles = -(-head.shape[1] // TILE)
+    bf16, f32 = jnp.bfloat16, jnp.float32
+    vmem = pl.BlockSpec(memory_space=pltpu.VMEM)
+    smem = pl.BlockSpec(memory_space=pltpu.SMEM)
+    hbm = pl.BlockSpec(memory_space=pl.ANY)
+    message = heads * rows + 2 * rows
+    dma = pltpu.SemaphoreType.DMA
+    return pl.pallas_call(
+        functools.partial(fused_kernel, n, tp),
+        out_shape=(
+            jax.ShapeDtypeStruct((1, rows), f32),
+            jax.ShapeDtypeStruct((1, rows, width), bf16),
+        ),
+        in_specs=[vmem, vmem, vmem, vmem, vmem, smem, vmem, vmem, smem, hbm, hbm],
+        out_specs=(vmem, vmem),
+        scratch_shapes=[
+            pltpu.VMEM(wo_sides.shape[1:], bf16),
+            pltpu.VMEM((head.shape[1], depth), bf16),
+            pltpu.VMEM((n, rows, width), bf16),
+            pltpu.VMEM((n, message, HEAD_SIZE), bf16),
+            pltpu.VMEM((n, message, HEAD_SIZE), bf16),
+            pltpu.VMEM((n, rows, width), bf16),
+            pltpu.VMEM((n, rows, width), bf16),
+            pltpu.VMEM((rows, width), bf16),
+            pltpu.VMEM((n, rows, width), bf16),
+            pltpu.VMEM((rows, width), f32),
+            pltpu.VMEM((rows, width), f32),
+            pltpu.VMEM((rows, HEAD_SIZE), f32),
+            pltpu.VMEM((n, rows, HEAD_SIZE), f32),
+            pltpu.VMEM((2 * rows, depth), bf16),
+            pltpu.VMEM((tiles, rows, TILE), f32),
+            pltpu.VMEM((tiles, rows, TILE), f32),
+            pltpu.VMEM((tiles, rows, TILE), f32),
+            pltpu.VMEM((rows, HEAD_SIZE), f32),
+            pltpu.VMEM((n, rows, HEAD_SIZE), f32),
+            dma,
+            dma((tiles,)),
+            dma((n,)),
+            dma((n,)),
+            dma((n,)),
+            dma((n,)),
+            dma((n,)),
+            dma((n,)),
+            dma((n,)),
+            dma((n,)),
+            dma((2,)),
+            dma((n,)),
+            dma((n,)),
+            dma((tiles,)),
+            dma((tiles,)),
+            dma((n,)),
+            dma((n,)),
+        ],
+        compiler_params=pltpu.CompilerParams(
+            collective_id=0, has_side_effects=True, vmem_limit_bytes=60 * 1024 * 1024
+        ),
+    )(
+        queries,
+        step_token_keys,
+        step_token_values,
+        stored_key_cache,
+        stored_value_cache,
+        lengths,
+        gain_sides,
+        resid,
+        actions,
+        wo_sides,
+        head.T,
+    )
+
+
+def on_device(*args):
+    queries, lengths, head = args[0], args[5], args[8]
+    n = lax.axis_size("grp") * lax.axis_size("tp")
+    width = queries.shape[2]
+    group = QUERY_HEADS // KEY_VALUE_HEADS
+    whole_heads = width % HEAD_SIZE == 0 and group % (width // HEAD_SIZE) == 0
+    fits = lax.axis_size("role") == 2 and n % 2 == 0 and lengths.shape[0] == 8
+    if whole_heads and fits and head.shape[0] == n * width and head.shape[1] > TILE:
+        return fused(*args)
+    return plain(*args)
+
+
 def solution(mesh):
     in_specs = (
         P(None, None, ("grp", "tp")),

time: 335 us -> 57.1 us (0.17)
  blocking collectives: 207 us -> 0 us
  waiting for transfers between devices: 67.8 us -> 0 us
  Pallas kernels: 0 us -> 53.8 us
  matrix products: 34.5 us -> 0 us
  between operations: 14.2 us -> 0.64 us
  other arithmetic: 3.38 us -> 0 us
    psum x2 -> x0, blocking collectives: 88.2 us -> none  [the longest x1 58.6 us: on_device(): totals = lax.psum(totals.reshape(count_of_rows, QUERY_HEADS), both)]
    reduce_scatter x2 -> x0, waiting for transfers between devices: 64.8 us -> none  [the longest x1 54.9 us: on_device(): lax.psum_scatter(jnp.dot(own_part, wo_sides[0], preferred_element_type=jn...]
    all_gather x3 -> x0, blocking collectives: 60.6 us -> none  [the longest x1 23.8 us: on_device(): lax.all_gather(lax.dynamic_index_in_dim(queries, step, 0, keepdims=False)...]
    pmax x1 -> x0, blocking collectives: 57.8 us -> none  [on_device(): lax.pmax(jnp.maximum(jnp.max(scores, axis=-1), fresh_highest), both)]
    pallas_call x0 -> x1, Pallas kernels: none -> 53.8 us  [fused(): pl.pallas_call(functools.partial(fused_kernel, n, tp), out_shape=(jax.Sha...]
    dot_general x6 -> x0, matrix products: 34.5 us -> none  [the longest x1 25.1 us: on_device(): jnp.dot(lax.all_gather(normed_now, both, axis=1, tiled=True), head, prefe...]
  transfers between devices with their start and end apart: 4 -> 0, of which waited for: 3 -> 0; matrix products, arithmetic and copies ran while one was open for 8% -> 0% of each run, Pallas kernels for 0% -> 0%
where the time goes in v2:
time: 57.1 us; the launch traced here: 56.8 us
  Pallas kernels  53.8 us (94%)
  local copies, waits for them, and re-layouts  2.43 us (4%)
  between operations  0.64 us (1%)
    pallas_call x1, Pallas kernels, fused(): pl.pallas_call(functools.partial(fused_kernel, n, tp), out_shape=(jax.Sha...  53.8 us
    unnamed x2, local copies, waits for them, and re-layouts  2.43 us

profile of v2, /device:TPU:0, one launch (start us, length us, event | category | flops | bytes accessed | tf_op | source)
XLA Modules:
  0.0 56.8 jit_solution(11575673525917462676)
XLA Ops:
  0.6 53.8 %shard_map.122 = (f32[1,8]{1,0:T(1,128)}, bf16[1,8,512]{2,1,0:T(8,128)(2,1)}) custom-call(bf16[2,8,512]{2,1,0:T(8,128)(2,1)} %queries.1, bf16[2,8,1024]{2,1,0:T(8,128)(2,1)} %token_keys.1, bf16[2,8,1024]{2,1,0:T(8,128)(2,1)} %token_values.1, bf16[8,32,1024]{2,1,0:T(8,128)(2,1)} %keys.1, bf16[8,32,1024]{2,1,0:T(8,128)(2,1)} %values.1, s32[8]{0:T(128)} %lengths.1, ...), custom_call_target="tpu_custom_call" | custom-call | tf_op jit(solution)/shard_map/pallas_call | solution.py:566
  54.4 1.1 %copy.15 = f32[1,8]{1,0:T(1,128)} copy(f32[1,8]{1,0:T(1,128)} %get-tuple-element.4) | data formatting | bytes 64
  55.5 1.3 %copy.16 = bf16[1,8,512]{2,1,0:T(8,128)(2,1)} copy(bf16[1,8,512]{2,1,0:T(8,128)(2,1)} %get-tuple-element.5) | data formatting | bytes 16384

commit v3 on v2

--- a/solution.py
+++ b/solution.py
@@ -124,8 +124,8 @@
     queries,
     token_keys,
     token_values,
-    keys,
-    values,
+    keys_in,
+    values_in,
     lengths,
     gain,
     resid,
@@ -134,6 +134,8 @@
     head,
     log_probs,
     normed,
+    keys,
+    values,
     wo_buf,
     head_buf,
     q_all,
@@ -153,6 +155,7 @@
     y_recv,
     e_send,
     e_recv,
+    kv_sems,
     wo_sem,
     head_sems,
     q_ss,
@@ -203,6 +206,10 @@
             device_id_type=MESH,
         )
 
+    key_copy = pltpu.make_async_copy(keys_in, keys, kv_sems.at[0])
+    value_copy = pltpu.make_async_copy(values_in, values, kv_sems.at[1])
+    key_copy.start()
+    value_copy.start()
     wo_copy = pltpu.make_async_copy(wo.at[0], wo_buf, wo_sem)
     wo_copy.start()
 
@@ -250,6 +257,9 @@
     def _(i):
         src = (me + i) % n
         remote(queries.at[step], q_all.at[src], q_ss.at[i], q_rs.at[src], role, me).wait_recv()
+
+    key_copy.wait()
+    value_copy.wait()
 
     lane = lax.broadcasted_iota(jnp.int32, (rows, HEAD_SIZE), 1)
     per_group = group // own_heads
@@ -569,9 +579,11 @@
             jax.ShapeDtypeStruct((1, rows), f32),
             jax.ShapeDtypeStruct((1, rows, width), bf16),
         ),
-        in_specs=[vmem, vmem, vmem, vmem, vmem, smem, vmem, vmem, smem, hbm, hbm],
+        in_specs=[vmem, vmem, vmem, hbm, hbm, smem, vmem, vmem, smem, hbm, hbm],
         out_specs=(vmem, vmem),
         scratch_shapes=[
+            pltpu.VMEM(stored_key_cache.shape, bf16),
+            pltpu.VMEM(stored_value_cache.shape, bf16),
             pltpu.VMEM(wo_sides.shape[1:], bf16),
             pltpu.VMEM((head.shape[1], depth), bf16),
             pltpu.VMEM((n, rows, width), bf16),
@@ -591,6 +603,7 @@
             pltpu.VMEM((tiles, rows, TILE), f32),
             pltpu.VMEM((rows, HEAD_SIZE), f32),
             pltpu.VMEM((n, rows, HEAD_SIZE), f32),
+            dma((2,)),
             dma,
             dma((tiles,)),
             dma((n,)),

time: 57.1 us -> 56.6 us (level)
  no operation moved by 1% of the time
where the time goes in v3:
time: 56.6 us; the launch traced here: 56.4 us
  Pallas kernels  53.3 us (94%)
  local copies, waits for them, and re-layouts  2.43 us (4%)
  between operations  0.64 us (1%)
    pallas_call x1, Pallas kernels, fused(): pl.pallas_call(functools.partial(fused_kernel, n, tp), out_shape=(jax.Sha...  53.3 us
    unnamed x2, local copies, waits for them, and re-layouts  2.43 us

profile of v3, /device:TPU:0, one launch (start us, length us, event | category | flops | bytes accessed | tf_op | source)
XLA Modules:
  0.0 56.4 jit_solution(12880741012277194088)
XLA Ops:
  0.6 53.3 %shard_map.122 = (f32[1,8]{1,0:T(1,128)}, bf16[1,8,512]{2,1,0:T(8,128)(2,1)}) custom-call(bf16[2,8,512]{2,1,0:T(8,128)(2,1)} %queries.1, bf16[2,8,1024]{2,1,0:T(8,128)(2,1)} %token_keys.1, bf16[2,8,1024]{2,1,0:T(8,128)(2,1)} %token_values.1, bf16[8,32,1024]{2,1,0:T(8,128)(2,1)} %keys_in.1, bf16[8,32,1024]{2,1,0:T(8,128)(2,1)} %values_in.1, s32[8]{0:T(128)} %lengths.1, ...), custom_call_target="tpu_custom_call" | custom-call | tf_op jit(solution)/shard_map/pallas_call | solution.py:576
  54.0 1.1 %copy.15 = f32[1,8]{1,0:T(1,128)} copy(f32[1,8]{1,0:T(1,128)} %get-tuple-element.4) | data formatting | bytes 64
  55.1 1.3 %copy.16 = bf16[1,8,512]{2,1,0:T(8,128)(2,1)} copy(bf16[1,8,512]{2,1,0:T(8,128)(2,1)} %get-tuple-element.5) | data formatting | bytes 16384
